TPU v7x, 32 devices: a whole 2x2x4 slice. The times are simulated.
32 devices in a mesh: groups: 2 (over y), blk: 4 (over z), tok: 4 (over x, core).
Axes of the slice: x: 2, y: 2, z: 4, core: 2. Of those that a mesh axis runs over, the one named last changes fastest.
Arguments:
- tokens: bfloat16 [2048, 3584], P(('groups', 'blk', 'tok')), parts along dimension 0, may hold values from -6 to 6
- expert_ids: int32 [2048, 1], P(('groups', 'blk', 'tok')), parts along dimension 0, may hold values from 0 to 1; in each aligned block of 256 rows (0 to 255, 256 to 511, ...) at most 192 rows name the same one
- gate_values: float32 [2048, 1], P(('groups', 'blk', 'tok')), parts along dimension 0, may hold values from 0.2 to 1
- w_gate: bfloat16 [2, 3584, 1024], P(None, 'blk', 'tok'), may hold values from -0.09375 to 0.09375
- w_up: bfloat16 [2, 3584, 1024], P(None, 'blk', 'tok'), may hold values from -0.09375 to 0.09375
- w_down: bfloat16 [2, 1024, 3584], P(None, 'tok', 'blk'), may hold values from -0.1875 to 0.1875
Outputs:
- mixed: bfloat16 [2048, 3584], P(('groups', 'blk', 'tok')), parts along dimension 0
There are 2 independent parts, one for each index of `groups`. A program takes and returns all parts, laid end to end along the dimension named above; an argument that names none is the same for every part. Nothing has to cross between parts.
Inputs may be any that keep to these rules, and one draw needn't show every extreme that they name: `expert_ids`: in each aligned block of 256 rows (the tokens of one index of blk), no expert is named by more than 192 rows, and in every draw some expert reaches 192 in some block.
All inputs are finite; a program needn't handle non-finite values.
Results may differ from a plain program's by a relative error of at most 0.005.
Values may be sent and summed in bfloat16 or wider, within the bound.
A program may use at most 64 MiB of HBM per device.

v0:
```python
import functools

import jax
import jax.numpy as jnp
from jax import lax
from jax.experimental import pallas as pl
from jax.experimental.pallas import tpu as pltpu
from jax.sharding import PartitionSpec as P

LANES = 128
SUBLANES = 8
CHUNKS = 1
WAVES = 2


def gathered_body(tokens, expert_ids, gate_values, w_gate, w_up, w_down):
    group_rows = lax.all_gather(tokens, "tok", axis=0, tiled=True)
    group_routes = lax.all_gather(expert_ids, "tok", axis=0, tiled=True)[:, 0]
    experts = w_gate.shape[0]
    count_rows = group_rows.shape[0]
    capacity = 3 * count_rows // 4
    expert_range = jnp.arange(experts, dtype=jnp.int32)
    onehot = (group_routes[:, None] == expert_range[None, :]).astype(jnp.int32)
    slot_rank = jnp.sum((jnp.cumsum(onehot, axis=0) - onehot) * onehot, axis=1)
    expert_match = group_routes[None, None, :] == expert_range[:, None, None]
    slot_match = slot_rank[None, None, :] == jnp.arange(capacity, dtype=jnp.int32)[None, :, None]
    dispatch = (expert_match & slot_match).astype(jnp.bfloat16)
    slots = jnp.einsum(
        "esg,gd->esd", dispatch, group_rows, preferred_element_type=jnp.float32
    ).astype(jnp.bfloat16)

    def add_part(weights):
        return jnp.einsum("esd,edf->esf", slots, weights, preferred_element_type=jnp.float32)

    gate_sum = add_part(lax.all_gather(w_gate, "blk", axis=1, tiled=True))
    up_sum = add_part(lax.all_gather(w_up, "blk", axis=1, tiled=True))
    hidden = (jax.nn.silu(gate_sum) * up_sum).astype(jnp.bfloat16)
    slot_out = jnp.einsum(
        "esf,efd->esd",
        hidden,
        lax.all_gather(w_down, "blk", axis=2, tiled=True),
        preferred_element_type=jnp.float32,
    )
    flat_rows = slot_out.reshape(experts * capacity, slot_out.shape[2])
    position = group_routes * capacity + slot_rank
    partial_value = jnp.take(flat_rows, position, axis=0)
    summed = lax.psum_scatter(partial_value, "tok", scatter_dimension=0, tiled=True)
    return (gate_values * summed).astype(jnp.bfloat16)


def kernel(
    nb, nt, tok_hbm, ids_ref, values_ref, wg_hbm, wu_hbm, wd_hbm, out_ref,
    tok, meta, wg, wu, wd, xs, part, part_send, part_recv, hid, ys, ycore, yx_send, yx_recv, fin_send,
    local_sem, z_send, z_recv, x_send, x_recv, c_send, c_recv, f_send, f_recv, m_send, m_recv,
    p_send, p_recv, h_send, h_recv, yc_send_sem, yc_recv_sem, yx_send_sem, yx_recv_sem, o_send, o_recv,
):
    g, b, t = lax.axis_index("groups"), lax.axis_index("blk"), lax.axis_index("tok")
    all_rows, width = tok.shape[0], xs.shape[4]
    rows = all_rows // WAVES
    experts, ff = wg.shape[0], wg.shape[2]
    half = nt // 2
    f32, bf16 = jnp.float32, jnp.bfloat16
    pair = t + 1 - 2 * lax.rem(t, 2)

    outer = lax.rem((b + 1) // 2 + 1, 2)
    piece = nt * rows // CHUNKS

    def blk(k):
        low, high = lax.rem(b, 2), b // 2
        low = 1 - low if k % 2 else low
        high = 1 - high if k // 2 else high
        return 2 * high + low

    def chunk(c):
        return pl.ds(c * piece, piece)

    def tk(base, j):
        return lax.rem(base + j + nt, nt)

    def cols(block):
        return pl.ds(pl.multiple_of(block * width, LANES), width)

    def remote(src, dst, send, recv, to_b, to_t):
        copy = pltpu.make_async_remote_copy(
            src_ref=src, dst_ref=dst, send_sem=send, recv_sem=recv,
            device_id=(g, to_b, to_t), device_id_type=pl.DeviceIdType.MESH,
        )
        copy.start()
        sends.append(copy)

    def arrived(dst, recv):
        pltpu.make_async_copy(dst, dst, recv).wait()

    sends = []
    own = [
        pltpu.make_async_copy(tok_hbm.at[pl.ds(w * rows, rows), cols(b)], xs.at[w, b, t], local_sem.at[5 + w])
        for w in range(WAVES)
    ]
    local = [
        pltpu.make_async_copy(tok_hbm, tok, local_sem.at[0]),
        None,
        pltpu.make_async_copy(wd_hbm, wd, local_sem.at[2]),
        pltpu.make_async_copy(wg_hbm, wg, local_sem.at[3]),
        pltpu.make_async_copy(wu_hbm, wu, local_sem.at[4]),
    ]
    for copy in own + local:
        if copy is not None:
            copy.start()

    meta[b, t] = jnp.zeros((SUBLANES, LANES), f32)
    meta[b, t, 0:1, :all_rows] = ids_ref[...].astype(f32)
    meta[b, t, 1:2, :all_rows] = values_ref[...]

    barrier = pltpu.get_barrier_semaphore()
    for k in range(nb):
        for j in range(nt):
            if k or j:
                pl.semaphore_signal(
                    barrier, inc=1, device_id=(g, blk(k), tk(t, j)),
                    device_id_type=pl.DeviceIdType.MESH,
                )
    pl.semaphore_wait(barrier, nb * nt - 1)

    order = list(range(nb))
    others = order[1:]

    local[0].wait()
    for k in others:
        remote(tok.at[pl.ds(0, rows), cols(blk(k))], xs.at[0, b, t], z_send.at[0, k], z_recv.at[0, k], blk(k), t)
    for k in order:
        for j in range(nt):
            if k or j:
                remote(meta.at[b, t], meta.at[b, t], m_send.at[k, j], m_recv.at[k, j], blk(k), tk(t, j))
    for w in range(1, WAVES):
        for k in others:
            remote(
                tok.at[pl.ds(w * rows, rows), cols(blk(k))], xs.at[w, b, t],
                z_send.at[w, k], z_recv.at[w, k], blk(k), t,
            )
    for copy in own:
        copy.wait()

    def spread(w, k):
        source = blk(k)
        if k:
            arrived(xs.at[w, source, t], z_recv.at[w, k])
        mine = xs.at[w, source, t]
        for j in range(1, half):
            remote(mine, mine, x_send.at[w, k, j], x_recv.at[w, k, j], b, tk(t, 2 * j))
        remote(mine, mine, c_send.at[w, k], c_recv.at[w, k], b, pair)

    def pass_on(w, k):
        source = blk(k)
        for j in range(1, half):
            theirs = xs.at[w, source, tk(t, -2 * j)]
            arrived(theirs, x_recv.at[w, k, j])
            remote(theirs, theirs, f_send.at[w, k, j], f_recv.at[w, k, j], b, pair)

    def column(w, k, row):
        flat = meta[blk(k)].reshape(nt * SUBLANES, LANES)
        turned = jnp.transpose(flat)
        return jnp.concatenate(
            [turned[w * rows:(w + 1) * rows, SUBLANES * i + row:SUBLANES * i + row + 1] for i in range(nt)], axis=0
        )

    def contract(w, k):
        source = blk(k)
        arrived(xs.at[w, source, pair], c_recv.at[w, k])
        for j in range(1, half):
            arrived(xs.at[w, source, tk(pair, -2 * j)], f_recv.at[w, k, j])
        for j in range(nt):
            if w == 0 and (k or j):
                arrived(meta.at[source, tk(t, -j)], m_recv.at[k, j])
        if k == 0 and w == 0:
            local[3].wait()
            local[4].wait()
        routes = column(w, k, 0)
        x = xs[w, source].reshape(nt * rows, width)
        for at, weights in ((0, wg), (ff, wu)):
            total = None
            for e in range(experts):
                value = jnp.dot(x, weights[e], preferred_element_type=f32)
                total = value if e == 0 else jnp.where(routes == e, value, total)
            part[w, k, :, at:at + ff] = total
        if k == 1:
            part_send[w, k] = part[w, k].astype(bf16)
            for c in range(CHUNKS):
                send_part(w, k, c).start()
        elif k:
            @pl.when(outer == 1)
            def _():
                part_send[w, k] = part[w, k].astype(bf16)
                for c in range(CHUNKS):
                    send_part(w, k, c).start()

    def send_part(w, k, c):
        slot = 0 if k == 1 else outer * (5 - k) + 1 - outer
        target = blk(1) if k == 1 else outer * blk(1) + (1 - outer) * blk(k)
        return pltpu.make_async_remote_copy(
            src_ref=part_send.at[w, k, chunk(c)], dst_ref=part_recv.at[w, slot, chunk(c)],
            send_sem=p_send.at[w, k, c], recv_sem=p_recv.at[w, slot, c],
            device_id=(g, target, t), device_id_type=pl.DeviceIdType.MESH,
        )

    def relay(w, k, c):
        @pl.when(outer == 0)
        def _():
            arrived(part_recv.at[w, k, chunk(c)], p_recv.at[w, k, c])
            part_send[w, k, chunk(c), :] = (part[w, k, chunk(c), :] + part_recv[w, k, chunk(c), :].astype(f32)).astype(bf16)
            send_part(w, k, c).start()

    def activate(w):
        values = column(w, 0, 1)
        for c in range(CHUNKS):
            total = part[w, 0, chunk(c), :]
            for slot in (0, 1):
                arrived(part_recv.at[w, slot, chunk(c)], p_recv.at[w, slot, c])
                total = total + part_recv[w, slot, chunk(c), :].astype(f32)
            gate, up = total[:, :ff], total[:, ff:]
            scale = values[c * piece:(c + 1) * piece]
            hid[w, b, chunk(c), :] = (gate / (1.0 + jnp.exp(-gate)) * up * scale).astype(bf16)
            for k in (2, 1):
                mine = hid.at[w, b, chunk(c)]
                remote(mine, mine, h_send.at[w, k, c], h_recv.at[w, k, c], blk(k), t)

    def forward(w, c):
        theirs = hid.at[w, blk(2), chunk(c)]
        arrived(theirs, h_recv.at[w, 2, c])
        remote(theirs, theirs, h_send.at[w, 3, c], h_recv.at[w, 3, c], blk(1), t)

    def expand(w, k):
        source = blk(k)
        if k == 0 and w == 0:
            local[2].wait()
        if k % 2:
            for c in range(CHUNKS):
                arrived(hid.at[w, source, chunk(c)], h_recv.at[w, k, c])
        if k == 1:
            for c in range(CHUNKS):
                forward(w, c)
        routes = column(w, k, 0)
        h = hid[w, source].astype(f32)
        routed = jnp.concatenate(
            [jnp.where(routes == e, h, 0.0).astype(bf16) for e in range(experts)], axis=1
        )
        ys[w, k] = jnp.dot(routed, wd[...].reshape(experts * ff, width), preferred_element_type=f32)
        for j in reversed(range(half)):
            remote(
                ys.at[w, k, rows_of(tk(pair, 2 * j))], ycore.at[w, k, j],
                yc_send_sem.at[w, k, j], yc_recv_sem.at[w, k, j], b, pair,
            )

    def rows_of(index):
        return pl.ds(pl.multiple_of(index * rows, SUBLANES), rows)

    def exchange(w, k):
        for j in range(1, half):
            arrived(ycore.at[w, k, j], yc_recv_sem.at[w, k, j])
            total = ys[w, k, rows_of(tk(t, 2 * j)), :] + ycore[w, k, j]
            yx_send[w, k, j] = total.astype(bf16)
            remote(
                yx_send.at[w, k, j], yx_recv.at[w, k, j],
                yx_send_sem.at[w, k, j], yx_recv_sem.at[w, k, j], b, tk(t, 2 * j),
            )

    def finish(w, k):
        arrived(ycore.at[w, k, 0], yc_recv_sem.at[w, k, 0])
        total = ys[w, k, rows_of(t), :] + ycore[w, k, 0]
        for j in range(1, half):
            arrived(yx_recv.at[w, k, j], yx_recv_sem.at[w, k, j])
            total = total + yx_recv[w, k, j].astype(f32)
        if k:
            fin_send[w, k] = total.astype(bf16)
            remote(fin_send.at[w, k], out_ref.at[pl.ds(w * rows, rows), cols(b)], o_send.at[w, k], o_recv.at[w, k], blk(k), t)
        else:
            out_ref[pl.ds(w * rows, rows), cols(b)] = total.astype(bf16)


    def pipeline(w, stage, fill=()):
        fill = list(fill)
        for step in range(nb + 2):
            for run, lag in stage:
                if 0 <= step - lag < nb:
                    run(w, order[step - lag])
            if fill and step >= 2:
                fill.pop(0)()
        for rest in fill:
            rest()

    def relay_block(w, k):
        for c in range(CHUNKS):
            relay(w, k, c)

    inward = [(spread, 0), (pass_on, 1), (contract, 2)]
    outward = [(expand, 0), (exchange, 1), (finish, 2)]
    for w in range(WAVES):
        fill = []
        if w:
            fill = [functools.partial(relay_block, w - 1, k) for k in (3, 2)]
            fill += [functools.partial(activate, w - 1)]
        pipeline(w, inward, fill)
    for k in (3, 2):
        relay_block(WAVES - 1, k)
    for w in range(WAVES):
        pipeline(w, outward, [functools.partial(activate, WAVES - 1)] if w == 0 else ())

    for w in range(WAVES):
        for k in others:
            arrived(out_ref.at[pl.ds(w * rows, rows), cols(blk(k))], o_recv.at[w, k])
    for copy in sends:
        copy.wait_send()
    for w in range(WAVES):
        for k in others:
            for c in range(CHUNKS):
                send_part(w, k, c).wait_send()


def stationary_body(nb, nt, tokens, expert_ids, gate_values, w_gate, w_up, w_down):
    rows, features = tokens.shape
    experts, width, ff = w_gate.shape
    f32, bf16 = jnp.float32, jnp.bfloat16
    wave_rows = rows // WAVES
    block, half = nt * wave_rows, nt // 2
    dma = pltpu.SemaphoreType.DMA
    vmem = pl.BlockSpec(memory_space=pltpu.VMEM)
    anywhere = pl.BlockSpec(memory_space=pl.ANY)
    return pl.pallas_call(
        functools.partial(kernel, nb, nt),
        out_shape=jax.ShapeDtypeStruct((rows, features), bf16),
        in_specs=[anywhere, vmem, vmem, anywhere, anywhere, anywhere],
        out_specs=vmem,
        scratch_shapes=[
            pltpu.VMEM((rows, features), bf16),
            pltpu.VMEM((nb, nt, SUBLANES, LANES), f32),
            pltpu.VMEM(w_gate.shape, bf16),
            pltpu.VMEM(w_up.shape, bf16),
            pltpu.VMEM(w_down.shape, bf16),
            pltpu.VMEM((WAVES, nb, nt, wave_rows, width), bf16),
            pltpu.VMEM((WAVES, nb, block, 2 * ff), f32),
            pltpu.VMEM((WAVES, nb, block, 2 * ff), bf16),
            pltpu.VMEM((WAVES, nb, block, 2 * ff), bf16),
            pltpu.VMEM((WAVES, nb, block, ff), bf16),
            pltpu.VMEM((WAVES, nb, block, width), f32),
            pltpu.VMEM((WAVES, nb, half, wave_rows, width), f32),
            pltpu.VMEM((WAVES, nb, half, wave_rows, width), bf16),
            pltpu.VMEM((WAVES, nb, half, wave_rows, width), bf16),
            pltpu.VMEM((WAVES, nb, wave_rows, width), bf16),
            dma((5 + WAVES,)),
            dma((WAVES, nb,)), dma((WAVES, nb,)),
            dma((WAVES, nb, half)), dma((WAVES, nb, half)),
            dma((WAVES, nb,)), dma((WAVES, nb,)),
            dma((WAVES, nb, half)), dma((WAVES, nb, half)),
            dma((nb, nt)), dma((nb, nt)),
            dma((WAVES, nb, CHUNKS)), dma((WAVES, nb, CHUNKS)),
            dma((WAVES, nb, CHUNKS)), dma((WAVES, nb, CHUNKS)),
            dma((WAVES, nb, half)), dma((WAVES, nb, half)),
            dma((WAVES, nb, half)), dma((WAVES, nb, half)),
            dma((WAVES, nb,)), dma((WAVES, nb,)),
        ],
        compiler_params=pltpu.CompilerParams(collective_id=0, has_side_effects=True),
    )(tokens, expert_ids.reshape(1, rows), gate_values.reshape(1, rows), w_gate, w_up, w_down)


def solution(mesh):
    nb, nt = mesh.shape["blk"], mesh.shape["tok"]

    def body(tokens, expert_ids, gate_values, w_gate, w_up, w_down):
        rows = tokens.shape[0]
        width, ff = w_gate.shape[1], w_gate.shape[2]
        fits = width % LANES == 0 and ff % LANES == 0 and rows % (16 * WAVES) == 0 and rows <= LANES
        if fits and nt % 2 == 0 and nb == 4 and nt * rows % (16 * CHUNKS * WAVES) == 0:
            return stationary_body(nb, nt, tokens, expert_ids, gate_values, w_gate, w_up, w_down)
        return gathered_body(tokens, expert_ids, gate_values, w_gate, w_up, w_down)

    return jax.shard_map(
        body,
        mesh=mesh,
        in_specs=(
            P(("groups", "blk", "tok"), None),
            P(("groups", "blk", "tok"), None),
            P(("groups", "blk", "tok"), None),
            P(None, "blk", "tok"),
            P(None, "blk", "tok"),
            P(None, "tok", "blk"),
        ),
        out_specs=P(("groups", "blk", "tok"), None),
        check_vma=False,
    )
```

profile of v0, /device:TPU:0, one launch (start us, length us, event | category | flops | bytes accessed | tf_op | source)
XLA Modules:
  0.0 70.3 jit_solution(1015480241233868911)
XLA Ops:
  0.0 68.5 %shard_map.64 = bf16[64,3584]{1,0:T(8,128)(2,1)} custom-call(bf16[64,3584]{1,0:T(8,128)(2,1)} %tok_hbm.1, s32[1,64]{1,0:T(1,128)} %bitcast.2, f32[1,64]{1,0:T(1,128)} %bitcast.3, bf16[2,896,256]{2,1,0:T(8,128)(2,1)} %wg_hbm.1, bf16[2,896,256]{2,1,0:T(8,128)(2,1)} %wu_hbm.1, bf16[2,256,896]{2,1,0:T(8,128)(2,1)} %wd_hbm.1), custom_call_target="tpu_custom_call" | custom-call | tf_op jit(solution)/shard_map/pallas_call | solution.py:327
  68.5 1.8 %copy.8 = bf16[64,3584]{1,0:T(8,128)(2,1)} copy(bf16[64,3584]{1,0:T(8,128)(2,1)} %shard_map.64) | data formatting | bytes 917504
where the time goes:
time: 70.5 us; the launch traced here: 70.3 us
  Pallas kernels  68.5 us (97%)
  local copies, waits for them, and re-layouts  1.82 us (3%)
    pallas_call x1, Pallas kernels, stationary_body(): pl.pallas_call(functools.partial(kernel, nb, nt), out_shape=jax.ShapeDtyp...  68.5 us
    unnamed x1, local copies, waits for them, and re-layouts  1.82 us

commit v1 on v0

v1 whole, which is shorter than its diff:
```python
import functools

import jax
import jax.numpy as jnp
from jax import lax
from jax.experimental import pallas as pl
from jax.experimental.pallas import tpu as pltpu
from jax.sharding import PartitionSpec as P

LANES = 128
SUBLANES = 8
WAVES = 2
ORDER = (
    ("Z", 0, 3), ("S", 1, 0), ("Z", 0, 1), ("S", 0, 0), ("Z", 0, 2), ("S", 0, 3),
    ("Z", 1, 3), ("S", 0, 2), ("Z", 1, 2), ("P", 0, 0), ("P", 0, 3), ("S", 0, 1),
    ("Z", 1, 1), ("C", 0, 0), ("C", 0, 3), ("P", 0, 2), ("S", 1, 3), ("C", 0, 2),
    ("S", 1, 2), ("P", 1, 3), ("P", 1, 0), ("P", 0, 1), ("R", 0, 2), ("C", 1, 3),
    ("S", 1, 1), ("P", 1, 2), ("C", 1, 2), ("C", 0, 1), ("R", 0, 3), ("R", 1, 2),
    ("C", 1, 0), ("R", 1, 3), ("P", 1, 1), ("C", 1, 1), ("A", 0, 0), ("A", 1, 0),
    ("H", 0, 3), ("E", 0, 0), ("E", 1, 0), ("H", 0, 2), ("E", 0, 2), ("H", 1, 3),
    ("E", 0, 3), ("X", 0, 2), ("E", 0, 1), ("X", 0, 3), ("X", 1, 0), ("H", 1, 2),
    ("E", 1, 1), ("E", 1, 3), ("F", 0, 2), ("X", 1, 3), ("F", 0, 3), ("E", 1, 2),
    ("X", 1, 1), ("X", 0, 1), ("X", 1, 2), ("X", 0, 0), ("F", 1, 3), ("F", 1, 1),
    ("F", 1, 0), ("F", 1, 2), ("F", 0, 0), ("F", 0, 1),
)


def gathered_body(tokens, expert_ids, gate_values, w_gate, w_up, w_down):
    group_rows = lax.all_gather(tokens, "tok", axis=0, tiled=True)
    group_routes = lax.all_gather(expert_ids, "tok", axis=0, tiled=True)[:, 0]
    experts = w_gate.shape[0]
    count_rows = group_rows.shape[0]
    capacity = 3 * count_rows // 4
    expert_range = jnp.arange(experts, dtype=jnp.int32)
    onehot = (group_routes[:, None] == expert_range[None, :]).astype(jnp.int32)
    slot_rank = jnp.sum((jnp.cumsum(onehot, axis=0) - onehot) * onehot, axis=1)
    expert_match = group_routes[None, None, :] == expert_range[:, None, None]
    slot_match = slot_rank[None, None, :] == jnp.arange(capacity, dtype=jnp.int32)[None, :, None]
    dispatch = (expert_match & slot_match).astype(jnp.bfloat16)
    slots = jnp.einsum(
        "esg,gd->esd", dispatch, group_rows, preferred_element_type=jnp.float32
    ).astype(jnp.bfloat16)

    def add_part(weights):
        return jnp.einsum("esd,edf->esf", slots, weights, preferred_element_type=jnp.float32)

    gate_sum = add_part(lax.all_gather(w_gate, "blk", axis=1, tiled=True))
    up_sum = add_part(lax.all_gather(w_up, "blk", axis=1, tiled=True))
    hidden = (jax.nn.silu(gate_sum) * up_sum).astype(jnp.bfloat16)
    slot_out = jnp.einsum(
        "esf,efd->esd",
        hidden,
        lax.all_gather(w_down, "blk", axis=2, tiled=True),
        preferred_element_type=jnp.float32,
    )
    flat_rows = slot_out.reshape(experts * capacity, slot_out.shape[2])
    position = group_routes * capacity + slot_rank
    partial_value = jnp.take(flat_rows, position, axis=0)
    summed = lax.psum_scatter(partial_value, "tok", scatter_dimension=0, tiled=True)
    return (gate_values * summed).astype(jnp.bfloat16)


def kernel(
    nb, nt, tok_hbm, ids_hbm, values_hbm, wg_hbm, wu_hbm, wd_hbm, out_ref,
    tok, ids, values, meta, wg, wu, wd, routes, scales, xs, part, part_send, part_recv, hid, ys, ycore,
    yx_send, yx_recv, fin_send,
    local_sem, send_sem, far, m_recv, z_recv, x_recv, c_recv, p_recv, h_recv, y_recv, yx_sem, o_recv,
):
    g, b, t = lax.axis_index("groups"), lax.axis_index("blk"), lax.axis_index("tok")
    all_rows, width = tok.shape[0], xs.shape[4]
    rows = all_rows // WAVES
    block = nt * rows
    experts, ff = wg.shape[0], wg.shape[2]
    f32, bf16 = jnp.float32, jnp.bfloat16
    pair = t + 1 - 2 * lax.rem(t, 2)
    across = lax.rem(t + 2, nt)
    across_pair = lax.rem(pair + 2, nt)
    outer = lax.rem((b + 1) // 2 + 1, 2) == 1
    inner = jnp.logical_not(outer)

    low, high = lax.rem(b, 2), b // 2
    blocks = [b, 2 * high + 1 - low, 2 * (1 - high) + low, 2 * (1 - high) + 1 - low]

    def blk(k):
        return blocks[k]

    def cols(index):
        return pl.ds(pl.multiple_of(index * width, LANES), width)

    def of_wave(w):
        return pl.ds(w * rows, rows)

    def noted(block_at, token_at):
        return block_at * nt + token_at

    def owned(index):
        return pl.ds(pl.multiple_of(index * rows, SUBLANES), rows)

    def remote(src, dst, kind, recv, to_b, to_t):
        pltpu.make_async_remote_copy(
            src_ref=src, dst_ref=dst, send_sem=send_sem.at[kind], recv_sem=recv,
            device_id=(g, to_b, to_t), device_id_type=pl.DeviceIdType.MESH,
        ).start()

    def arrived(dst, recv):
        pltpu.make_async_copy(dst, dst, recv).wait()

    def signal(sem, to_b, to_t):
        pl.semaphore_signal(sem, inc=1, device_id=(g, to_b, to_t), device_id_type=pl.DeviceIdType.MESH)

    own = [
        pltpu.make_async_copy(tok_hbm.at[of_wave(w), cols(b)], xs.at[w, b, t], local_sem.at[4])
        for w in range(WAVES)
    ]
    local = [
        pltpu.make_async_copy(tok_hbm, tok, local_sem.at[0]),
        pltpu.make_async_copy(wg_hbm, wg, local_sem.at[1]),
        pltpu.make_async_copy(wu_hbm, wu, local_sem.at[2]),
        pltpu.make_async_copy(wd_hbm, wd, local_sem.at[3]),
    ]
    notes = [
        pltpu.make_async_copy(ids_hbm, ids, local_sem.at[5]),
        pltpu.make_async_copy(values_hbm, values, local_sem.at[6]),
    ]
    barrier = pltpu.get_barrier_semaphore()
    signal(barrier, b, pair)
    signal(barrier, b, across)
    signal(barrier, blk(1), t)

    @pl.when(inner)
    def _():
        signal(barrier, blk(3), t)

    for copy in notes + local[:1] + own + local[1:]:
        copy.start()
    for copy in notes:
        copy.wait()
    meta[noted(b, t)] = jnp.zeros((SUBLANES, LANES), f32)
    meta[noted(b, t), 0:1, :all_rows] = ids[...].astype(f32)
    meta[noted(b, t), 1:2, :all_rows] = values[...]

    @pl.when(inner)
    def _():
        pl.semaphore_wait(barrier, 4)
        signal(far.at[0], blk(1), t)
        signal(far.at[0], blk(3), t)

    @pl.when(outer)
    def _():
        pl.semaphore_wait(barrier, 3)

    local[0].wait()
    arrived(fin_send.at[:, 0], local_sem.at[4])

    def far_known():
        pl.semaphore_wait(far.at[0], 1)

        @pl.when(inner)
        def _():
            signal(far.at[1], blk(1), t)

    def far_end():
        @pl.when(outer)
        def _():
            pl.semaphore_wait(far.at[1], 1)

    ready = {"weights": False, "down": False, "far": False, "end": False}

    def launch(w, k):
        if k == 2 and not ready["far"]:
            far_known()
            ready["far"] = True
        if k == 3 and not ready["end"]:
            far_end()
            ready["end"] = True
        if w == 0:
            note = meta.at[noted(b, t)]
            remote(note, note, 9, m_recv.at[0, k], blk(k), t)
        remote(tok.at[of_wave(w), cols(blk(k))], xs.at[w, b, t], 0, z_recv.at[w, k - 1], blk(k), t)

    def spread(w, k):
        source = blk(k)
        mine = xs.at[w, source, t]
        if w == 0:
            note = meta.at[noted(source, t)]
            if k:
                arrived(note, m_recv.at[0, k])
            remote(note, note, 9, m_recv.at[1, k], b, across)
            remote(note, note, 9, m_recv.at[2, k], b, pair)
        if k:
            arrived(mine, z_recv.at[w, k - 1])
        remote(mine, mine, 1, x_recv.at[w, k], b, across)
        remote(mine, mine, 2, c_recv.at[w, k], b, pair)

    def pass_on(w, k):
        source = blk(k)
        theirs = xs.at[w, source, across]
        if w == 0:
            note = meta.at[noted(source, across)]
            arrived(note, m_recv.at[1, k])
            remote(note, note, 9, m_recv.at[2, k], b, pair)
        arrived(theirs, x_recv.at[w, k])
        remote(theirs, theirs, 2, c_recv.at[w, k], b, pair)

    def wide(mask, size):
        return jnp.concatenate([mask] * (size // LANES), axis=1)

    def prepare(k):
        source = blk(k)
        arrived(meta.at[pl.ds(0, 2)], m_recv.at[2, k])
        turned = jnp.transpose(meta[pl.ds(source * nt, nt)].reshape(nt * SUBLANES, LANES))
        for row, out in ((0, routes),) if k else ((0, routes), (1, scales)):
            for w in range(WAVES):
                column = jnp.concatenate(
                    [turned[w * rows:(w + 1) * rows, SUBLANES * i + row:SUBLANES * i + row + 1] for i in range(nt)],
                    axis=0,
                )
                out[w, k] = jnp.broadcast_to(column, (block, LANES))

    def contract(w, k):
        source = blk(k)
        if w == 0:
            prepare(k)
        arrived(xs.at[w, source, pl.ds(0, 2)], c_recv.at[w, k])
        if not ready["weights"]:
            local[1].wait()
            local[2].wait()
            ready["weights"] = True
        chosen = wide(routes[w, k], ff)
        x = xs[w, source].reshape(block, width)
        for at, weights in ((0, wg), (ff, wu)):
            total = None
            for e in range(experts):
                value = jnp.dot(x, weights[e], preferred_element_type=f32)
                total = value if e == 0 else jnp.where(chosen == e, value, total)
            part[w, k, :, at:at + ff] = total
            if k:
                part_send[w, k, :, at:at + ff] = total.astype(bf16)
        if k == 1:
            remote(part_send.at[w, 1], part_recv.at[w, 0], 6, p_recv.at[w, 0], blk(1), t)
        elif k:
            @pl.when(outer)
            def _():
                remote(part_send.at[w, k], part_recv.at[w, 5 - k], 6, p_recv.at[w, 5 - k], blk(1), t)

    def relay(w, k):
        @pl.when(inner)
        def _():
            arrived(part_recv.at[w, k], p_recv.at[w, k])
            part_send[w, k] = (part[w, k] + part_recv[w, k].astype(f32)).astype(bf16)
            remote(part_send.at[w, k], part_recv.at[w, 1], 6, p_recv.at[w, 1], blk(k), t)

    def activate(w, k):
        total = part[w, 0]
        for slot in (0, 1):
            arrived(part_recv.at[w, slot], p_recv.at[w, slot])
            total = total + part_recv[w, slot].astype(f32)
        gate, up = total[:, :ff], total[:, ff:]
        hid[w, b] = (gate / (1.0 + jnp.exp(-gate)) * up * wide(scales[w, 0], ff)).astype(bf16)
        mine = hid.at[w, b]

        @pl.when(inner)
        def _():
            remote(mine, mine, 7, h_recv.at[w, 2], blk(3), t)

        remote(mine, mine, 7, h_recv.at[w, 0], blk(1), t)

        @pl.when(outer)
        def _():
            remote(mine, mine, 7, h_recv.at[w, 1], blk(2), t)

    def forward(w, k):
        @pl.when(inner)
        def _():
            source = blk(k)
            theirs = hid.at[w, source]
            arrived(theirs, h_recv.at[w, k - 1])
            if k == 1:
                remote(theirs, theirs, 8, h_recv.at[w, 1], blk(3), t)
            else:
                remote(theirs, theirs, 8, h_recv.at[w, 4 - k], blk(1), t)

    def expand(w, k):
        source = blk(k)
        if not ready["down"]:
            local[3].wait()
            ready["down"] = True
        if k:
            if k in (2, 3):
                @pl.when(outer)
                def _():
                    arrived(hid.at[w, source], h_recv.at[w, k - 1])
            else:
                arrived(hid.at[w, source], h_recv.at[w, k - 1])
        chosen = wide(routes[w, k], ff)
        h = hid[w, source].astype(f32)
        routed = jnp.concatenate([jnp.where(chosen == e, h, 0.0).astype(bf16) for e in range(experts)], axis=1)
        ys[w, k] = jnp.dot(routed, wd[...].reshape(experts * ff, width), preferred_element_type=f32)
        for j, place in ((1, across_pair), (0, pair)):
            remote(ys.at[w, k, owned(place)], ycore.at[w, k, j], 3, y_recv.at[w, k], b, pair)

    def exchange(w, k):
        arrived(ycore.at[w, k], y_recv.at[w, k])
        yx_send[w, k] = (ys[w, k, owned(across), :] + ycore[w, k, 1]).astype(bf16)
        remote(yx_send.at[w, k], yx_recv.at[w, k], 4, yx_sem.at[w, k], b, across)

    def finish(w, k):
        total = ys[w, k, owned(t), :] + ycore[w, k, 0]
        arrived(yx_recv.at[w, k], yx_sem.at[w, k])
        total = total + yx_recv[w, k].astype(f32)
        if k:
            fin_send[w, k] = total.astype(bf16)
            remote(fin_send.at[w, k], out_ref.at[of_wave(w), cols(b)], 5, o_recv.at[0], blk(k), t)
        else:
            out_ref[of_wave(w), cols(b)] = total.astype(bf16)

    steps = {
        "Z": launch, "S": spread, "P": pass_on, "C": contract, "R": relay,
        "A": activate, "H": forward, "E": expand, "X": exchange, "F": finish,
    }
    for name, w, k in ORDER:
        steps[name](w, k)

    others = fin_send.at[:, pl.ds(1, nb - 1)]
    arrived(others, o_recv.at[0])
    for kind, ref in (
        (0, others), (1, yx_send), (2, xs.at[:, :, pl.ds(0, 2)]), (3, ycore), (4, yx_send), (5, others),
        (6, part_send.at[:, pl.ds(1, nb - 1)]), (9, meta.at[pl.ds(0, nb * nt - 1)]),
    ):
        arrived(ref, send_sem.at[kind])

    @pl.when(inner)
    def _():
        arrived(hid.at[:, pl.ds(0, 2)], send_sem.at[7])
        arrived(hid.at[:, pl.ds(0, 2)], send_sem.at[8])

    @pl.when(outer)
    def _():
        arrived(hid.at[:, pl.ds(0, 2)], send_sem.at[7])


def stationary_body(nb, nt, tokens, expert_ids, gate_values, w_gate, w_up, w_down):
    rows, features = tokens.shape
    experts, width, ff = w_gate.shape
    f32, bf16 = jnp.float32, jnp.bfloat16
    wave_rows = rows // WAVES
    block = nt * wave_rows
    dma = pltpu.SemaphoreType.DMA
    vmem = pl.BlockSpec(memory_space=pltpu.VMEM)
    hbm = pl.BlockSpec(memory_space=pltpu.HBM)
    each = (WAVES, nb)
    return pl.pallas_call(
        functools.partial(kernel, nb, nt),
        out_shape=jax.ShapeDtypeStruct((rows, features), bf16),
        in_specs=[hbm] * 6,
        out_specs=vmem,
        scratch_shapes=[
            pltpu.VMEM((rows, features), bf16),
            pltpu.VMEM((1, rows), jnp.int32),
            pltpu.VMEM((1, rows), f32),
            pltpu.VMEM((nb * nt, SUBLANES, LANES), f32),
            pltpu.VMEM(w_gate.shape, bf16),
            pltpu.VMEM(w_up.shape, bf16),
            pltpu.VMEM(w_down.shape, bf16),
            pltpu.VMEM((*each, block, LANES), f32),
            pltpu.VMEM((WAVES, 1, block, LANES), f32),
            pltpu.VMEM((*each, nt, wave_rows, width), bf16),
            pltpu.VMEM((*each, block, 2 * ff), f32),
            pltpu.VMEM((*each, block, 2 * ff), bf16),
            pltpu.VMEM((*each, block, 2 * ff), bf16),
            pltpu.VMEM((*each, block, ff), bf16),
            pltpu.VMEM((*each, block, width), f32),
            pltpu.VMEM((*each, 2, wave_rows, width), f32),
            pltpu.VMEM((*each, wave_rows, width), bf16),
            pltpu.VMEM((*each, wave_rows, width), bf16),
            pltpu.VMEM((*each, wave_rows, width), bf16),
            dma((7,)),
            dma((10,)),
            pltpu.SemaphoreType.REGULAR((2,)),
            dma((3, nb)),
            dma((WAVES, nb - 1)), dma(each), dma(each), dma(each), dma((WAVES, nb - 1)), dma(each), dma(each), dma((1,)),
        ],
        compiler_params=pltpu.CompilerParams(
            collective_id=0, has_side_effects=True, vmem_limit_bytes=57000000,
        ),
    )(tokens, expert_ids.reshape(1, rows), gate_values.reshape(1, rows), w_gate, w_up, w_down)


def solution(mesh):
    nb, nt = mesh.shape["blk"], mesh.shape["tok"]

    def body(tokens, expert_ids, gate_values, w_gate, w_up, w_down):
        rows = tokens.shape[0]
        width, ff = w_gate.shape[1], w_gate.shape[2]
        fits = width % LANES == 0 and ff % LANES == 0 and rows % (16 * WAVES) == 0 and rows <= LANES
        if fits and nt == 4 and nb == 4:
            return stationary_body(nb, nt, tokens, expert_ids, gate_values, w_gate, w_up, w_down)
        return gathered_body(tokens, expert_ids, gate_values, w_gate, w_up, w_down)

    return jax.shard_map(
        body,
        mesh=mesh,
        in_specs=(
            P(("groups", "blk", "tok"), None),
            P(("groups", "blk", "tok"), None),
            P(("groups", "blk", "tok"), None),
            P(None, "blk", "tok"),
            P(None, "blk", "tok"),
            P(None, "tok", "blk"),
        ),
        out_specs=P(("groups", "blk", "tok"), None),
        check_vma=False,
    )
```

time: 70.5 us -> 60 us (0.85)
  Pallas kernels: 68.5 us -> 58 us
    pallas_call x1, Pallas kernels: 68.5 us -> 58 us  [stationary_body(): pl.pallas_call(functools.partial(kernel, nb, nt), out_shape=jax.ShapeDtyp...]
where the time goes in v1:
time: 60 us; the launch traced here: 59.8 us
  Pallas kernels  58 us (97%)
  local copies, waits for them, and re-layouts  1.82 us (3%)
    pallas_call x1, Pallas kernels, stationary_body(): pl.pallas_call(functools.partial(kernel, nb, nt), out_shape=jax.ShapeDtyp...  58 us
    unnamed x1, local copies, waits for them, and re-layouts  1.82 us

profile of v1, /device:TPU:0, one launch (start us, length us, event | category | flops | bytes accessed | tf_op | source)
XLA Modules:
  0.0 59.8 jit_solution(12387623063723615392)
XLA Ops:
  0.0 58.0 %shard_map.64 = bf16[64,3584]{1,0:T(8,128)(2,1)} custom-call(bf16[64,3584]{1,0:T(8,128)(2,1)} %tok_hbm.1, s32[1,64]{1,0:T(1,128)} %bitcast.2, f32[1,64]{1,0:T(1,128)} %bitcast.3, bf16[2,896,256]{2,1,0:T(8,128)(2,1)} %wg_hbm.1, bf16[2,896,256]{2,1,0:T(8,128)(2,1)} %wu_hbm.1, bf16[2,256,896]{2,1,0:T(8,128)(2,1)} %wd_hbm.1), custom_call_target="tpu_custom_call" | custom-call | tf_op jit(solution)/shard_map/pallas_call | solution.py:352
  58.0 1.8 %copy.8 = bf16[64,3584]{1,0:T(8,128)(2,1)} copy(bf16[64,3584]{1,0:T(8,128)(2,1)} %shard_map.64) | data formatting | bytes 917504

commit v2 on v1

--- a/solution.py
+++ b/solution.py
@@ -351,7 +351,7 @@
     each = (WAVES, nb)
     return pl.pallas_call(
         functools.partial(kernel, nb, nt),
-        out_shape=jax.ShapeDtypeStruct((rows, features), bf16),
+        out_shape=pltpu.VMEM((rows, features), bf16),
         in_specs=[hbm] * 6,
         out_specs=vmem,
         scratch_shapes=[
@@ -381,7 +381,7 @@
             dma((WAVES, nb - 1)), dma(each), dma(each), dma(each), dma((WAVES, nb - 1)), dma(each), dma(each), dma((1,)),
         ],
         compiler_params=pltpu.CompilerParams(
-            collective_id=0, has_side_effects=True, vmem_limit_bytes=57000000,
+            collective_id=0, has_side_effects=True, vmem_limit_bytes=60000000,
         ),
     )(tokens, expert_ids.reshape(1, rows), gate_values.reshape(1, rows), w_gate, w_up, w_down)
 

time: 60 us -> 58.1 us (0.968)
  local copies, waits for them, and re-layouts: 1.82 us -> 0.77 us
  Pallas kernels: 58 us -> 57.2 us
    unnamed x1, local copies, waits for them, and re-layouts: 1.82 us -> 0.77 us
    pallas_call x1, Pallas kernels: 58 us -> 57.2 us  [stationary_body(): pl.pallas_call(functools.partial(kernel, nb, nt), out_shape=pltpu.VMEM((r...]
where the time goes in v2:
time: 58.1 us; the launch traced here: 58 us
  Pallas kernels  57.2 us (98%)
  local copies, waits for them, and re-layouts  0.77 us (1%)
    pallas_call x1, Pallas kernels, stationary_body(): pl.pallas_call(functools.partial(kernel, nb, nt), out_shape=pltpu.VMEM((r...  57.2 us

profile of v2, /device:TPU:0, one launch (start us, length us, event | category | flops | bytes accessed | tf_op | source)
XLA Modules:
  0.0 58.0 jit_solution(17988906439869641842)
XLA Ops:
  0.0 57.2 %shard_map.64 = bf16[64,3584]{1,0:T(8,128)(2,1)S(1)} custom-call(bf16[64,3584]{1,0:T(8,128)(2,1)} %tok_hbm.1, s32[1,64]{1,0:T(1,128)} %bitcast.2, f32[1,64]{1,0:T(1,128)} %bitcast.3, bf16[2,896,256]{2,1,0:T(8,128)(2,1)} %wg_hbm.1, bf16[2,896,256]{2,1,0:T(8,128)(2,1)} %wu_hbm.1, bf16[2,256,896]{2,1,0:T(8,128)(2,1)} %wd_hbm.1), custom_call_target="tpu_custom_call" | custom-call | tf_op jit(solution)/shard_map/pallas_call | solution.py:352
  57.2 0.8 %copy.8 = bf16[64,3584]{1,0:T(8,128)(2,1)} copy(bf16[64,3584]{1,0:T(8,128)(2,1)S(1)} %shard_map.64) | data formatting | bytes 917504

commit v3 on v2

--- a/solution.py
+++ b/solution.py
@@ -9,19 +9,45 @@
 
 LANES = 128
 SUBLANES = 8
-WAVES = 2
-ORDER = (
-    ("Z", 0, 3), ("S", 1, 0), ("Z", 0, 1), ("S", 0, 0), ("Z", 0, 2), ("S", 0, 3),
-    ("Z", 1, 3), ("S", 0, 2), ("Z", 1, 2), ("P", 0, 0), ("P", 0, 3), ("S", 0, 1),
-    ("Z", 1, 1), ("C", 0, 0), ("C", 0, 3), ("P", 0, 2), ("S", 1, 3), ("C", 0, 2),
-    ("S", 1, 2), ("P", 1, 3), ("P", 1, 0), ("P", 0, 1), ("R", 0, 2), ("C", 1, 3),
-    ("S", 1, 1), ("P", 1, 2), ("C", 1, 2), ("C", 0, 1), ("R", 0, 3), ("R", 1, 2),
-    ("C", 1, 0), ("R", 1, 3), ("P", 1, 1), ("C", 1, 1), ("A", 0, 0), ("A", 1, 0),
-    ("H", 0, 3), ("E", 0, 0), ("E", 1, 0), ("H", 0, 2), ("E", 0, 2), ("H", 1, 3),
-    ("E", 0, 3), ("X", 0, 2), ("E", 0, 1), ("X", 0, 3), ("X", 1, 0), ("H", 1, 2),
-    ("E", 1, 1), ("E", 1, 3), ("F", 0, 2), ("X", 1, 3), ("F", 0, 3), ("E", 1, 2),
-    ("X", 1, 1), ("X", 0, 1), ("X", 1, 2), ("X", 0, 0), ("F", 1, 3), ("F", 1, 1),
-    ("F", 1, 0), ("F", 1, 2), ("F", 0, 0), ("F", 0, 1),
+WAVES = 4
+OUTER_ORDER = (
+    ("S", 0, 0), ("Z", 0, 1), ("Z", 2, 1), ("S", 1, 0), ("Z", 1, 1), ("S", 2, 0), ("Z", 3, 1),
+    ("S", 3, 0), ("Z", 1, 2), ("Z", 2, 2), ("P", 0, 0), ("Z", 1, 3), ("S", 0, 1), ("Z", 0, 3),
+    ("Z", 3, 3), ("Z", 2, 3), ("P", 1, 0), ("C", 0, 0), ("P", 2, 0), ("Z", 0, 2), ("C", 1, 0),
+    ("P", 3, 0), ("S", 1, 2), ("C", 2, 0), ("S", 3, 2), ("P", 0, 1), ("C", 3, 0), ("Z", 3, 2),
+    ("C", 0, 1), ("P", 1, 2), ("S", 1, 3), ("S", 0, 3), ("P", 3, 2), ("C", 1, 2), ("S", 0, 2),
+    ("S", 3, 3), ("C", 3, 2), ("S", 2, 3), ("P", 1, 3), ("P", 0, 3), ("C", 1, 3), ("S", 1, 1),
+    ("P", 0, 2), ("C", 0, 3), ("C", 0, 2), ("P", 3, 3), ("P", 2, 3), ("C", 3, 3), ("C", 2, 3),
+    ("P", 1, 1), ("S", 3, 1), ("C", 1, 1), ("S", 2, 2), ("S", 2, 1), ("P", 3, 1), ("P", 2, 2),
+    ("C", 3, 1), ("A", 1, 0), ("C", 2, 2), ("P", 2, 1), ("E", 1, 0), ("A", 0, 0), ("E", 0, 0),
+    ("C", 2, 1), ("X", 1, 0), ("X", 0, 0), ("A", 3, 0), ("E", 3, 0), ("E", 0, 1), ("F", 0, 0),
+    ("X", 3, 0), ("A", 2, 0), ("E", 2, 0), ("E", 1, 1), ("X", 0, 1), ("E", 3, 1), ("X", 2, 0),
+    ("X", 1, 1), ("X", 3, 1), ("F", 3, 0), ("E", 0, 2), ("E", 1, 2), ("F", 0, 1), ("X", 0, 2),
+    ("F", 2, 0), ("E", 3, 2), ("F", 1, 1), ("X", 1, 2), ("E", 1, 3), ("F", 3, 1), ("X", 3, 2),
+    ("F", 1, 0), ("X", 1, 3), ("E", 2, 1), ("F", 0, 2), ("E", 0, 3), ("X", 2, 1), ("F", 1, 2),
+    ("E", 3, 3), ("X", 0, 3), ("F", 3, 2), ("E", 2, 3), ("F", 1, 3), ("X", 3, 3), ("E", 2, 2),
+    ("X", 2, 3), ("F", 2, 1), ("X", 2, 2), ("F", 0, 3), ("F", 3, 3), ("F", 2, 3), ("F", 2, 2),
+)
+INNER_ORDER = (
+    ("Z", 1, 3), ("Z", 3, 3), ("S", 2, 0), ("S", 1, 0), ("Z", 0, 1), ("S", 3, 0), ("S", 0, 0),
+    ("Z", 1, 2), ("Z", 3, 2), ("S", 1, 3), ("S", 0, 1), ("P", 2, 0), ("S", 3, 3), ("S", 2, 1),
+    ("P", 1, 0), ("C", 2, 0), ("S", 1, 1), ("P", 3, 0), ("C", 1, 0), ("P", 0, 0), ("S", 3, 1),
+    ("Z", 0, 2), ("C", 3, 0), ("P", 1, 3), ("S", 1, 2), ("C", 0, 0), ("P", 0, 1), ("S", 2, 2),
+    ("C", 1, 3), ("P", 3, 3), ("C", 0, 1), ("Z", 1, 1), ("P", 2, 1), ("P", 1, 1), ("C", 3, 3),
+    ("Z", 0, 3), ("P", 3, 1), ("C", 2, 1), ("C", 1, 1), ("Z", 3, 1), ("C", 3, 1), ("Z", 2, 3),
+    ("S", 0, 2), ("P", 1, 2), ("P", 2, 2), ("S", 3, 2), ("C", 1, 2), ("C", 2, 2), ("S", 0, 3),
+    ("Z", 2, 2), ("R", 1, 3), ("S", 2, 3), ("P", 0, 2), ("P", 3, 2), ("C", 0, 2), ("Z", 2, 1),
+    ("R", 3, 3), ("C", 3, 2), ("P", 0, 3), ("R", 1, 2), ("P", 2, 3), ("C", 0, 3), ("C", 2, 3),
+    ("R", 0, 2), ("R", 0, 3), ("R", 3, 2), ("R", 2, 2), ("A", 0, 0), ("E", 0, 0), ("A", 1, 0),
+    ("E", 1, 0), ("X", 0, 0), ("A", 3, 0), ("E", 3, 0), ("X", 1, 0), ("H", 1, 1), ("E", 1, 1),
+    ("X", 3, 0), ("X", 1, 1), ("R", 2, 3), ("H", 0, 3), ("E", 0, 3), ("H", 0, 1), ("E", 0, 1),
+    ("H", 1, 3), ("E", 1, 3), ("F", 1, 0), ("X", 0, 3), ("H", 3, 3), ("E", 3, 3), ("X", 0, 1),
+    ("F", 3, 0), ("H", 1, 2), ("E", 1, 2), ("X", 1, 3), ("H", 3, 1), ("E", 3, 1), ("X", 3, 3),
+    ("F", 1, 1), ("H", 2, 1), ("E", 2, 1), ("X", 1, 2), ("A", 2, 0), ("E", 2, 0), ("X", 3, 1),
+    ("H", 0, 2), ("F", 0, 3), ("E", 0, 2), ("X", 2, 1), ("F", 0, 1), ("X", 2, 0), ("F", 1, 3),
+    ("H", 3, 2), ("E", 3, 2), ("X", 0, 2), ("F", 3, 3), ("H", 2, 2), ("E", 2, 2), ("X", 3, 2),
+    ("F", 0, 0), ("H", 2, 3), ("E", 2, 3), ("F", 3, 1), ("X", 2, 2), ("F", 1, 2), ("F", 2, 1),
+    ("X", 2, 3), ("F", 2, 0), ("F", 0, 2), ("F", 3, 2), ("F", 2, 2), ("F", 2, 3),
 )
 
 
@@ -152,28 +178,31 @@
     local[0].wait()
     arrived(fin_send.at[:, 0], local_sem.at[4])
 
-    def far_known():
-        pl.semaphore_wait(far.at[0], 1)
-
-        @pl.when(inner)
-        def _():
-            signal(far.at[1], blk(1), t)
-
-    def far_end():
-        @pl.when(outer)
-        def _():
+    ready = set()
+
+    def once(*name):
+        if name in ready:
+            return False
+        ready.add(name)
+        return True
+
+    def only(side):
+        def call(step):
+            if side in ready:
+                step()
+        return call
+
+    def announced(k):
+        if k == 2 and once("far"):
+            pl.semaphore_wait(far.at[0], 1)
+            if "inner" in ready:
+                signal(far.at[1], blk(1), t)
+        if k == 3 and "outer" in ready and once("end"):
             pl.semaphore_wait(far.at[1], 1)
 
-    ready = {"weights": False, "down": False, "far": False, "end": False}
-
     def launch(w, k):
-        if k == 2 and not ready["far"]:
-            far_known()
-            ready["far"] = True
-        if k == 3 and not ready["end"]:
-            far_end()
-            ready["end"] = True
-        if w == 0:
+        announced(k)
+        if once("launch", k):
             note = meta.at[noted(b, t)]
             remote(note, note, 9, m_recv.at[0, k], blk(k), t)
         remote(tok.at[of_wave(w), cols(blk(k))], xs.at[w, b, t], 0, z_recv.at[w, k - 1], blk(k), t)
@@ -181,7 +210,7 @@
     def spread(w, k):
         source = blk(k)
         mine = xs.at[w, source, t]
-        if w == 0:
+        if once("spread", k):
             note = meta.at[noted(source, t)]
             if k:
                 arrived(note, m_recv.at[0, k])
@@ -195,7 +224,7 @@
     def pass_on(w, k):
         source = blk(k)
         theirs = xs.at[w, source, across]
-        if w == 0:
+        if once("pass", k):
             note = meta.at[noted(source, across)]
             arrived(note, m_recv.at[1, k])
             remote(note, note, 9, m_recv.at[2, k], b, pair)
@@ -219,13 +248,12 @@
 
     def contract(w, k):
         source = blk(k)
-        if w == 0:
+        if once("note", k):
             prepare(k)
         arrived(xs.at[w, source, pl.ds(0, 2)], c_recv.at[w, k])
-        if not ready["weights"]:
+        if once("up"):
             local[1].wait()
             local[2].wait()
-            ready["weights"] = True
         chosen = wide(routes[w, k], ff)
         x = xs[w, source].reshape(block, width)
         for at, weights in ((0, wg), (ff, wu)):
@@ -239,12 +267,12 @@
         if k == 1:
             remote(part_send.at[w, 1], part_recv.at[w, 0], 6, p_recv.at[w, 0], blk(1), t)
         elif k:
-            @pl.when(outer)
+            @only("outer")
             def _():
                 remote(part_send.at[w, k], part_recv.at[w, 5 - k], 6, p_recv.at[w, 5 - k], blk(1), t)
 
     def relay(w, k):
-        @pl.when(inner)
+        @only("inner")
         def _():
             arrived(part_recv.at[w, k], p_recv.at[w, k])
             part_send[w, k] = (part[w, k] + part_recv[w, k].astype(f32)).astype(bf16)
@@ -259,18 +287,14 @@
         hid[w, b] = (gate / (1.0 + jnp.exp(-gate)) * up * wide(scales[w, 0], ff)).astype(bf16)
         mine = hid.at[w, b]
 
-        @pl.when(inner)
+        @only("inner")
         def _():
             remote(mine, mine, 7, h_recv.at[w, 2], blk(3), t)
 
         remote(mine, mine, 7, h_recv.at[w, 0], blk(1), t)
 
-        @pl.when(outer)
-        def _():
-            remote(mine, mine, 7, h_recv.at[w, 1], blk(2), t)
-
     def forward(w, k):
-        @pl.when(inner)
+        @only("inner")
         def _():
             source = blk(k)
             theirs = hid.at[w, source]
@@ -282,12 +306,11 @@
 
     def expand(w, k):
         source = blk(k)
-        if not ready["down"]:
+        if once("down"):
             local[3].wait()
-            ready["down"] = True
         if k:
-            if k in (2, 3):
-                @pl.when(outer)
+            if k in (1, 2, 3):
+                @only("outer")
                 def _():
                     arrived(hid.at[w, source], h_recv.at[w, k - 1])
             else:
@@ -318,25 +341,37 @@
         "Z": launch, "S": spread, "P": pass_on, "C": contract, "R": relay,
         "A": activate, "H": forward, "E": expand, "X": exchange, "F": finish,
     }
-    for name, w, k in ORDER:
-        steps[name](w, k)
-
-    others = fin_send.at[:, pl.ds(1, nb - 1)]
-    arrived(others, o_recv.at[0])
-    for kind, ref in (
-        (0, others), (1, yx_send), (2, xs.at[:, :, pl.ds(0, 2)]), (3, ycore), (4, yx_send), (5, others),
-        (6, part_send.at[:, pl.ds(1, nb - 1)]), (9, meta.at[pl.ds(0, nb * nt - 1)]),
-    ):
-        arrived(ref, send_sem.at[kind])
+    def run(side, order):
+        ready.clear()
+        ready.add(side)
+        for name, w, k in order:
+            if side == "inner" and name != "Z" and (name, k) != ("S", 0):
+                announced(2)
+            steps[name](w, k)
+        others = fin_send.at[:, pl.ds(1, nb - 1)]
+        arrived(others, o_recv.at[0])
+        for kind, ref in (
+            (0, others), (1, yx_send), (2, xs.at[:, :, pl.ds(0, 2)]), (3, ycore), (4, yx_send), (5, others),
+            (6, part_send.at[:, pl.ds(1, nb - 1)]), (9, meta.at[pl.ds(0, nb * nt - 1)]),
+        ):
+            arrived(ref, send_sem.at[kind])
+
+        @only("inner")
+        def _():
+            arrived(hid.at[:, pl.ds(0, 2)], send_sem.at[7])
+            arrived(hid.at[:, pl.ds(0, 3)], send_sem.at[8])
+
+        @only("outer")
+        def _():
+            arrived(hid.at[:, pl.ds(0, 1)], send_sem.at[7])
 
     @pl.when(inner)
     def _():
-        arrived(hid.at[:, pl.ds(0, 2)], send_sem.at[7])
-        arrived(hid.at[:, pl.ds(0, 2)], send_sem.at[8])
+        run("inner", INNER_ORDER)
 
     @pl.when(outer)
     def _():
-        arrived(hid.at[:, pl.ds(0, 2)], send_sem.at[7])
+        run("outer", OUTER_ORDER)
 
 
 def stationary_body(nb, nt, tokens, expert_ids, gate_values, w_gate, w_up, w_down):
@@ -346,14 +381,13 @@
     wave_rows = rows // WAVES
     block = nt * wave_rows
     dma = pltpu.SemaphoreType.DMA
-    vmem = pl.BlockSpec(memory_space=pltpu.VMEM)
     hbm = pl.BlockSpec(memory_space=pltpu.HBM)
     each = (WAVES, nb)
     return pl.pallas_call(
         functools.partial(kernel, nb, nt),
         out_shape=pltpu.VMEM((rows, features), bf16),
         in_specs=[hbm] * 6,
-        out_specs=vmem,
+        out_specs=pl.BlockSpec(memory_space=pltpu.VMEM),
         scratch_shapes=[
             pltpu.VMEM((rows, features), bf16),
             pltpu.VMEM((1, rows), jnp.int32),
@@ -381,7 +415,7 @@
             dma((WAVES, nb - 1)), dma(each), dma(each), dma(each), dma((WAVES, nb - 1)), dma(each), dma(each), dma((1,)),
         ],
         compiler_params=pltpu.CompilerParams(
-            collective_id=0, has_side_effects=True, vmem_limit_bytes=60000000,
+            collective_id=0, has_side_effects=True, vmem_limit_bytes=60_000_000,
         ),
     )(tokens, expert_ids.reshape(1, rows), gate_values.reshape(1, rows), w_gate, w_up, w_down)
 

time: 58.1 us -> 55.7 us (0.959)
  Pallas kernels: 57.2 us -> 54.8 us
    pallas_call x1, Pallas kernels: 57.2 us -> 54.8 us  [stationary_body(): pl.pallas_call(functools.partial(kernel, nb, nt), out_shape=pltpu.VMEM((r...]
where the time goes in v3:
time: 55.7 us; the launch traced here: 55.6 us
  Pallas kernels  54.8 us (98%)
  local copies, waits for them, and re-layouts  0.77 us (1%)
    pallas_call x1, Pallas kernels, stationary_body(): pl.pallas_call(functools.partial(kernel, nb, nt), out_shape=pltpu.VMEM((r...  54.8 us

profile of v3, /device:TPU:0, one launch (start us, length us, event | category | flops | bytes accessed | tf_op | source)
XLA Modules:
  0.0 55.6 jit_solution(10139579067275542291)
XLA Ops:
  0.0 54.8 %shard_map.64 = bf16[64,3584]{1,0:T(8,128)(2,1)S(1)} custom-call(bf16[64,3584]{1,0:T(8,128)(2,1)} %tok_hbm.1, s32[1,64]{1,0:T(1,128)} %bitcast.2, f32[1,64]{1,0:T(1,128)} %bitcast.3, bf16[2,896,256]{2,1,0:T(8,128)(2,1)} %wg_hbm.1, bf16[2,896,256]{2,1,0:T(8,128)(2,1)} %wu_hbm.1, bf16[2,256,896]{2,1,0:T(8,128)(2,1)} %wd_hbm.1), custom_call_target="tpu_custom_call" | custom-call | tf_op jit(solution)/shard_map/pallas_call | solution.py:386
  54.8 0.8 %copy.8 = bf16[64,3584]{1,0:T(8,128)(2,1)} copy(bf16[64,3584]{1,0:T(8,128)(2,1)S(1)} %shard_map.64) | data formatting | bytes 917504

commit v4 on v3

--- a/solution.py
+++ b/solution.py
@@ -11,43 +11,43 @@
 SUBLANES = 8
 WAVES = 4
 OUTER_ORDER = (
-    ("S", 0, 0), ("Z", 0, 1), ("Z", 2, 1), ("S", 1, 0), ("Z", 1, 1), ("S", 2, 0), ("Z", 3, 1),
-    ("S", 3, 0), ("Z", 1, 2), ("Z", 2, 2), ("P", 0, 0), ("Z", 1, 3), ("S", 0, 1), ("Z", 0, 3),
-    ("Z", 3, 3), ("Z", 2, 3), ("P", 1, 0), ("C", 0, 0), ("P", 2, 0), ("Z", 0, 2), ("C", 1, 0),
-    ("P", 3, 0), ("S", 1, 2), ("C", 2, 0), ("S", 3, 2), ("P", 0, 1), ("C", 3, 0), ("Z", 3, 2),
-    ("C", 0, 1), ("P", 1, 2), ("S", 1, 3), ("S", 0, 3), ("P", 3, 2), ("C", 1, 2), ("S", 0, 2),
-    ("S", 3, 3), ("C", 3, 2), ("S", 2, 3), ("P", 1, 3), ("P", 0, 3), ("C", 1, 3), ("S", 1, 1),
-    ("P", 0, 2), ("C", 0, 3), ("C", 0, 2), ("P", 3, 3), ("P", 2, 3), ("C", 3, 3), ("C", 2, 3),
-    ("P", 1, 1), ("S", 3, 1), ("C", 1, 1), ("S", 2, 2), ("S", 2, 1), ("P", 3, 1), ("P", 2, 2),
-    ("C", 3, 1), ("A", 1, 0), ("C", 2, 2), ("P", 2, 1), ("E", 1, 0), ("A", 0, 0), ("E", 0, 0),
-    ("C", 2, 1), ("X", 1, 0), ("X", 0, 0), ("A", 3, 0), ("E", 3, 0), ("E", 0, 1), ("F", 0, 0),
-    ("X", 3, 0), ("A", 2, 0), ("E", 2, 0), ("E", 1, 1), ("X", 0, 1), ("E", 3, 1), ("X", 2, 0),
-    ("X", 1, 1), ("X", 3, 1), ("F", 3, 0), ("E", 0, 2), ("E", 1, 2), ("F", 0, 1), ("X", 0, 2),
-    ("F", 2, 0), ("E", 3, 2), ("F", 1, 1), ("X", 1, 2), ("E", 1, 3), ("F", 3, 1), ("X", 3, 2),
-    ("F", 1, 0), ("X", 1, 3), ("E", 2, 1), ("F", 0, 2), ("E", 0, 3), ("X", 2, 1), ("F", 1, 2),
-    ("E", 3, 3), ("X", 0, 3), ("F", 3, 2), ("E", 2, 3), ("F", 1, 3), ("X", 3, 3), ("E", 2, 2),
-    ("X", 2, 3), ("F", 2, 1), ("X", 2, 2), ("F", 0, 3), ("F", 3, 3), ("F", 2, 3), ("F", 2, 2),
+    ("S", 2, 0), ("Z", 2, 1), ("S", 3, 0), ("Z", 0, 1), ("Z", 3, 1), ("S", 1, 0), ("S", 0, 0),
+    ("Z", 2, 2), ("Z", 1, 3), ("Z", 2, 3), ("Z", 3, 3), ("Z", 0, 3), ("S", 3, 1), ("P", 2, 0),
+    ("P", 3, 0), ("C", 2, 0), ("P", 1, 0), ("C", 3, 0), ("P", 0, 0), ("S", 0, 2), ("Z", 1, 1),
+    ("C", 1, 0), ("C", 0, 0), ("Z", 1, 2), ("P", 3, 1), ("S", 2, 2), ("Z", 3, 2), ("C", 3, 1),
+    ("S", 1, 3), ("Z", 0, 2), ("S", 2, 3), ("P", 0, 2), ("S", 3, 3), ("C", 0, 2), ("P", 2, 2),
+    ("S", 0, 3), ("S", 3, 2), ("C", 2, 2), ("P", 1, 3), ("S", 2, 1), ("P", 2, 3), ("C", 1, 3),
+    ("P", 3, 3), ("C", 2, 3), ("S", 0, 1), ("P", 0, 3), ("C", 3, 3), ("P", 3, 2), ("C", 0, 3),
+    ("P", 2, 1), ("C", 3, 2), ("C", 2, 1), ("P", 0, 1), ("S", 1, 2), ("C", 0, 1), ("S", 1, 1),
+    ("P", 1, 2), ("A", 1, 0), ("E", 1, 0), ("P", 1, 1), ("C", 1, 2), ("A", 2, 0), ("E", 2, 0),
+    ("C", 1, 1), ("X", 1, 0), ("A", 3, 0), ("E", 3, 0), ("X", 2, 0), ("A", 0, 0), ("E", 0, 0),
+    ("X", 3, 0), ("E", 2, 1), ("X", 0, 0), ("F", 2, 0), ("X", 2, 1), ("E", 0, 1), ("X", 0, 1),
+    ("E", 3, 1), ("E", 2, 2), ("F", 0, 0), ("X", 3, 1), ("F", 3, 0), ("F", 2, 1), ("E", 0, 2),
+    ("X", 2, 2), ("E", 1, 3), ("F", 0, 1), ("X", 0, 2), ("E", 3, 2), ("X", 1, 3), ("F", 3, 1),
+    ("X", 3, 2), ("E", 1, 1), ("E", 2, 3), ("F", 2, 2), ("X", 1, 1), ("E", 3, 3), ("F", 0, 2),
+    ("X", 2, 3), ("F", 1, 3), ("E", 0, 3), ("X", 3, 3), ("F", 1, 0), ("F", 3, 2), ("E", 1, 2),
+    ("X", 0, 3), ("F", 1, 1), ("X", 1, 2), ("F", 2, 3), ("F", 3, 3), ("F", 0, 3), ("F", 1, 2),
 )
 INNER_ORDER = (
-    ("Z", 1, 3), ("Z", 3, 3), ("S", 2, 0), ("S", 1, 0), ("Z", 0, 1), ("S", 3, 0), ("S", 0, 0),
-    ("Z", 1, 2), ("Z", 3, 2), ("S", 1, 3), ("S", 0, 1), ("P", 2, 0), ("S", 3, 3), ("S", 2, 1),
-    ("P", 1, 0), ("C", 2, 0), ("S", 1, 1), ("P", 3, 0), ("C", 1, 0), ("P", 0, 0), ("S", 3, 1),
-    ("Z", 0, 2), ("C", 3, 0), ("P", 1, 3), ("S", 1, 2), ("C", 0, 0), ("P", 0, 1), ("S", 2, 2),
-    ("C", 1, 3), ("P", 3, 3), ("C", 0, 1), ("Z", 1, 1), ("P", 2, 1), ("P", 1, 1), ("C", 3, 3),
-    ("Z", 0, 3), ("P", 3, 1), ("C", 2, 1), ("C", 1, 1), ("Z", 3, 1), ("C", 3, 1), ("Z", 2, 3),
-    ("S", 0, 2), ("P", 1, 2), ("P", 2, 2), ("S", 3, 2), ("C", 1, 2), ("C", 2, 2), ("S", 0, 3),
-    ("Z", 2, 2), ("R", 1, 3), ("S", 2, 3), ("P", 0, 2), ("P", 3, 2), ("C", 0, 2), ("Z", 2, 1),
-    ("R", 3, 3), ("C", 3, 2), ("P", 0, 3), ("R", 1, 2), ("P", 2, 3), ("C", 0, 3), ("C", 2, 3),
-    ("R", 0, 2), ("R", 0, 3), ("R", 3, 2), ("R", 2, 2), ("A", 0, 0), ("E", 0, 0), ("A", 1, 0),
-    ("E", 1, 0), ("X", 0, 0), ("A", 3, 0), ("E", 3, 0), ("X", 1, 0), ("H", 1, 1), ("E", 1, 1),
-    ("X", 3, 0), ("X", 1, 1), ("R", 2, 3), ("H", 0, 3), ("E", 0, 3), ("H", 0, 1), ("E", 0, 1),
-    ("H", 1, 3), ("E", 1, 3), ("F", 1, 0), ("X", 0, 3), ("H", 3, 3), ("E", 3, 3), ("X", 0, 1),
-    ("F", 3, 0), ("H", 1, 2), ("E", 1, 2), ("X", 1, 3), ("H", 3, 1), ("E", 3, 1), ("X", 3, 3),
-    ("F", 1, 1), ("H", 2, 1), ("E", 2, 1), ("X", 1, 2), ("A", 2, 0), ("E", 2, 0), ("X", 3, 1),
-    ("H", 0, 2), ("F", 0, 3), ("E", 0, 2), ("X", 2, 1), ("F", 0, 1), ("X", 2, 0), ("F", 1, 3),
-    ("H", 3, 2), ("E", 3, 2), ("X", 0, 2), ("F", 3, 3), ("H", 2, 2), ("E", 2, 2), ("X", 3, 2),
-    ("F", 0, 0), ("H", 2, 3), ("E", 2, 3), ("F", 3, 1), ("X", 2, 2), ("F", 1, 2), ("F", 2, 1),
-    ("X", 2, 3), ("F", 2, 0), ("F", 0, 2), ("F", 3, 2), ("F", 2, 2), ("F", 2, 3),
+    ("Z", 3, 1), ("S", 2, 0), ("Z", 2, 3), ("Z", 0, 3), ("S", 1, 0), ("S", 0, 0), ("S", 3, 0),
+    ("Z", 0, 2), ("Z", 2, 2), ("P", 2, 0), ("S", 2, 3), ("S", 2, 1), ("S", 0, 1), ("P", 1, 0),
+    ("S", 0, 3), ("C", 2, 0), ("Z", 1, 3), ("S", 3, 1), ("Z", 3, 3), ("P", 0, 0), ("C", 1, 0),
+    ("P", 3, 0), ("C", 0, 0), ("Z", 3, 2), ("C", 3, 0), ("S", 2, 2), ("P", 2, 3), ("P", 2, 1),
+    ("C", 2, 3), ("P", 0, 1), ("Z", 2, 1), ("C", 2, 1), ("S", 1, 3), ("Z", 0, 1), ("P", 0, 3),
+    ("P", 3, 1), ("S", 1, 1), ("C", 0, 1), ("S", 3, 3), ("C", 0, 3), ("C", 3, 1), ("P", 2, 2),
+    ("S", 1, 2), ("C", 2, 2), ("S", 3, 2), ("P", 1, 3), ("P", 1, 1), ("C", 1, 3), ("P", 3, 3),
+    ("Z", 1, 2), ("C", 1, 1), ("S", 0, 2), ("R", 0, 3), ("C", 3, 3), ("P", 1, 2), ("Z", 1, 1),
+    ("P", 3, 2), ("R", 2, 3), ("C", 1, 2), ("C", 3, 2), ("R", 1, 2), ("P", 0, 2), ("R", 2, 2),
+    ("C", 0, 2), ("R", 3, 2), ("R", 0, 2), ("R", 3, 3), ("A", 2, 0), ("E", 2, 0), ("A", 0, 0),
+    ("X", 2, 0), ("E", 0, 0), ("H", 1, 1), ("E", 1, 1), ("X", 0, 0), ("A", 3, 0), ("E", 3, 0),
+    ("X", 1, 1), ("R", 1, 3), ("H", 2, 3), ("E", 2, 3), ("H", 2, 1), ("E", 2, 1), ("X", 3, 0),
+    ("X", 2, 3), ("H", 0, 3), ("E", 0, 3), ("X", 2, 1), ("H", 1, 2), ("E", 1, 2), ("H", 3, 1),
+    ("E", 3, 1), ("X", 0, 3), ("H", 3, 3), ("E", 3, 3), ("H", 0, 1), ("E", 0, 1), ("X", 1, 2),
+    ("F", 1, 1), ("X", 3, 1), ("X", 3, 3), ("A", 1, 0), ("E", 1, 0), ("F", 0, 0), ("X", 0, 1),
+    ("F", 3, 0), ("F", 2, 3), ("H", 2, 2), ("E", 2, 2), ("X", 1, 0), ("H", 3, 2), ("E", 3, 2),
+    ("F", 2, 0), ("F", 0, 3), ("X", 2, 2), ("H", 0, 2), ("E", 0, 2), ("F", 1, 2), ("X", 3, 2),
+    ("H", 1, 3), ("E", 1, 3), ("F", 2, 1), ("F", 3, 3), ("X", 0, 2), ("F", 0, 1), ("X", 1, 3),
+    ("F", 3, 1), ("F", 1, 0), ("F", 2, 2), ("F", 3, 2), ("F", 0, 2), ("F", 1, 3),
 )
 
 

time: 55.7 us -> 54.3 us (0.975)
  Pallas kernels: 54.8 us -> 53.3 us
    pallas_call x1, Pallas kernels: 54.8 us -> 53.3 us  [stationary_body(): pl.pallas_call(functools.partial(kernel, nb, nt), out_shape=pltpu.VMEM((r...]
where the time goes in v4:
time: 54.3 us; the launch traced here: 54.1 us
  Pallas kernels  53.3 us (98%)
  local copies, waits for them, and re-layouts  0.77 us (1%)
    pallas_call x1, Pallas kernels, stationary_body(): pl.pallas_call(functools.partial(kernel, nb, nt), out_shape=pltpu.VMEM((r...  53.3 us

profile of v4, /device:TPU:0, one launch (start us, length us, event | category | flops | bytes accessed | tf_op | source)
XLA Modules:
  0.0 54.1 jit_solution(13803124483510910686)
XLA Ops:
  0.0 53.3 %shard_map.64 = bf16[64,3584]{1,0:T(8,128)(2,1)S(1)} custom-call(bf16[64,3584]{1,0:T(8,128)(2,1)} %tok_hbm.1, s32[1,64]{1,0:T(1,128)} %bitcast.2, f32[1,64]{1,0:T(1,128)} %bitcast.3, bf16[2,896,256]{2,1,0:T(8,128)(2,1)} %wg_hbm.1, bf16[2,896,256]{2,1,0:T(8,128)(2,1)} %wu_hbm.1, bf16[2,256,896]{2,1,0:T(8,128)(2,1)} %wd_hbm.1), custom_call_target="tpu_custom_call" | custom-call | tf_op jit(solution)/shard_map/pallas_call | solution.py:386
  53.4 0.8 %copy.8 = bf16[64,3584]{1,0:T(8,128)(2,1)} copy(bf16[64,3584]{1,0:T(8,128)(2,1)S(1)} %shard_map.64) | data formatting | bytes 917504

commit v5 on v4

--- a/solution.py
+++ b/solution.py
@@ -11,43 +11,43 @@
 SUBLANES = 8
 WAVES = 4
 OUTER_ORDER = (
-    ("S", 2, 0), ("Z", 2, 1), ("S", 3, 0), ("Z", 0, 1), ("Z", 3, 1), ("S", 1, 0), ("S", 0, 0),
-    ("Z", 2, 2), ("Z", 1, 3), ("Z", 2, 3), ("Z", 3, 3), ("Z", 0, 3), ("S", 3, 1), ("P", 2, 0),
-    ("P", 3, 0), ("C", 2, 0), ("P", 1, 0), ("C", 3, 0), ("P", 0, 0), ("S", 0, 2), ("Z", 1, 1),
-    ("C", 1, 0), ("C", 0, 0), ("Z", 1, 2), ("P", 3, 1), ("S", 2, 2), ("Z", 3, 2), ("C", 3, 1),
-    ("S", 1, 3), ("Z", 0, 2), ("S", 2, 3), ("P", 0, 2), ("S", 3, 3), ("C", 0, 2), ("P", 2, 2),
-    ("S", 0, 3), ("S", 3, 2), ("C", 2, 2), ("P", 1, 3), ("S", 2, 1), ("P", 2, 3), ("C", 1, 3),
-    ("P", 3, 3), ("C", 2, 3), ("S", 0, 1), ("P", 0, 3), ("C", 3, 3), ("P", 3, 2), ("C", 0, 3),
-    ("P", 2, 1), ("C", 3, 2), ("C", 2, 1), ("P", 0, 1), ("S", 1, 2), ("C", 0, 1), ("S", 1, 1),
-    ("P", 1, 2), ("A", 1, 0), ("E", 1, 0), ("P", 1, 1), ("C", 1, 2), ("A", 2, 0), ("E", 2, 0),
-    ("C", 1, 1), ("X", 1, 0), ("A", 3, 0), ("E", 3, 0), ("X", 2, 0), ("A", 0, 0), ("E", 0, 0),
-    ("X", 3, 0), ("E", 2, 1), ("X", 0, 0), ("F", 2, 0), ("X", 2, 1), ("E", 0, 1), ("X", 0, 1),
-    ("E", 3, 1), ("E", 2, 2), ("F", 0, 0), ("X", 3, 1), ("F", 3, 0), ("F", 2, 1), ("E", 0, 2),
-    ("X", 2, 2), ("E", 1, 3), ("F", 0, 1), ("X", 0, 2), ("E", 3, 2), ("X", 1, 3), ("F", 3, 1),
-    ("X", 3, 2), ("E", 1, 1), ("E", 2, 3), ("F", 2, 2), ("X", 1, 1), ("E", 3, 3), ("F", 0, 2),
-    ("X", 2, 3), ("F", 1, 3), ("E", 0, 3), ("X", 3, 3), ("F", 1, 0), ("F", 3, 2), ("E", 1, 2),
-    ("X", 0, 3), ("F", 1, 1), ("X", 1, 2), ("F", 2, 3), ("F", 3, 3), ("F", 0, 3), ("F", 1, 2),
+    ("S", 2, 0), ("S", 0, 0), ("Z", 0, 1), ("Z", 1, 1), ("Z", 2, 1), ("S", 3, 0), ("S", 1, 0),
+    ("Z", 3, 1), ("Z", 3, 3), ("Z", 0, 3), ("Z", 2, 3), ("Z", 1, 3), ("P", 2, 0), ("S", 2, 1),
+    ("P", 0, 0), ("C", 2, 0), ("Z", 3, 2), ("P", 3, 0), ("C", 0, 0), ("S", 1, 2), ("Z", 0, 2),
+    ("P", 1, 0), ("C", 3, 0), ("S", 3, 2), ("Z", 2, 2), ("Z", 1, 2), ("C", 1, 0), ("P", 2, 1),
+    ("S", 3, 3), ("C", 2, 1), ("S", 0, 3), ("P", 1, 2), ("S", 2, 3), ("S", 1, 3), ("P", 3, 2),
+    ("C", 1, 2), ("S", 2, 2), ("S", 3, 1), ("C", 3, 2), ("P", 3, 3), ("P", 0, 3), ("C", 3, 3),
+    ("P", 2, 3), ("C", 0, 3), ("P", 1, 3), ("P", 2, 2), ("C", 2, 3), ("S", 1, 1), ("P", 3, 1),
+    ("C", 1, 3), ("C", 2, 2), ("C", 3, 1), ("S", 0, 2), ("P", 1, 1), ("C", 1, 1), ("P", 0, 2),
+    ("S", 0, 1), ("C", 0, 2), ("A", 3, 0), ("E", 3, 0), ("P", 0, 1), ("A", 0, 0), ("X", 3, 0),
+    ("E", 0, 0), ("C", 0, 1), ("A", 2, 0), ("E", 2, 0), ("X", 0, 0), ("A", 1, 0), ("E", 1, 0),
+    ("X", 2, 0), ("F", 3, 0), ("E", 3, 1), ("X", 1, 0), ("X", 3, 1), ("E", 1, 1), ("X", 1, 1),
+    ("F", 2, 0), ("E", 2, 1), ("E", 3, 2), ("X", 2, 1), ("F", 3, 1), ("E", 1, 2), ("X", 3, 2),
+    ("F", 1, 1), ("X", 1, 2), ("E", 0, 1), ("E", 2, 2), ("F", 2, 1), ("X", 0, 1), ("E", 3, 3),
+    ("F", 3, 2), ("X", 2, 2), ("E", 0, 3), ("F", 1, 2), ("X", 3, 3), ("E", 2, 3), ("X", 0, 3),
+    ("E", 1, 3), ("X", 2, 3), ("F", 0, 0), ("E", 0, 2), ("F", 0, 1), ("X", 1, 3), ("F", 1, 0),
+    ("F", 2, 2), ("X", 0, 2), ("F", 3, 3), ("F", 0, 3), ("F", 2, 3), ("F", 1, 3), ("F", 0, 2),
 )
 INNER_ORDER = (
-    ("Z", 3, 1), ("S", 2, 0), ("Z", 2, 3), ("Z", 0, 3), ("S", 1, 0), ("S", 0, 0), ("S", 3, 0),
-    ("Z", 0, 2), ("Z", 2, 2), ("P", 2, 0), ("S", 2, 3), ("S", 2, 1), ("S", 0, 1), ("P", 1, 0),
-    ("S", 0, 3), ("C", 2, 0), ("Z", 1, 3), ("S", 3, 1), ("Z", 3, 3), ("P", 0, 0), ("C", 1, 0),
-    ("P", 3, 0), ("C", 0, 0), ("Z", 3, 2), ("C", 3, 0), ("S", 2, 2), ("P", 2, 3), ("P", 2, 1),
-    ("C", 2, 3), ("P", 0, 1), ("Z", 2, 1), ("C", 2, 1), ("S", 1, 3), ("Z", 0, 1), ("P", 0, 3),
-    ("P", 3, 1), ("S", 1, 1), ("C", 0, 1), ("S", 3, 3), ("C", 0, 3), ("C", 3, 1), ("P", 2, 2),
-    ("S", 1, 2), ("C", 2, 2), ("S", 3, 2), ("P", 1, 3), ("P", 1, 1), ("C", 1, 3), ("P", 3, 3),
-    ("Z", 1, 2), ("C", 1, 1), ("S", 0, 2), ("R", 0, 3), ("C", 3, 3), ("P", 1, 2), ("Z", 1, 1),
-    ("P", 3, 2), ("R", 2, 3), ("C", 1, 2), ("C", 3, 2), ("R", 1, 2), ("P", 0, 2), ("R", 2, 2),
-    ("C", 0, 2), ("R", 3, 2), ("R", 0, 2), ("R", 3, 3), ("A", 2, 0), ("E", 2, 0), ("A", 0, 0),
-    ("X", 2, 0), ("E", 0, 0), ("H", 1, 1), ("E", 1, 1), ("X", 0, 0), ("A", 3, 0), ("E", 3, 0),
-    ("X", 1, 1), ("R", 1, 3), ("H", 2, 3), ("E", 2, 3), ("H", 2, 1), ("E", 2, 1), ("X", 3, 0),
-    ("X", 2, 3), ("H", 0, 3), ("E", 0, 3), ("X", 2, 1), ("H", 1, 2), ("E", 1, 2), ("H", 3, 1),
-    ("E", 3, 1), ("X", 0, 3), ("H", 3, 3), ("E", 3, 3), ("H", 0, 1), ("E", 0, 1), ("X", 1, 2),
-    ("F", 1, 1), ("X", 3, 1), ("X", 3, 3), ("A", 1, 0), ("E", 1, 0), ("F", 0, 0), ("X", 0, 1),
-    ("F", 3, 0), ("F", 2, 3), ("H", 2, 2), ("E", 2, 2), ("X", 1, 0), ("H", 3, 2), ("E", 3, 2),
-    ("F", 2, 0), ("F", 0, 3), ("X", 2, 2), ("H", 0, 2), ("E", 0, 2), ("F", 1, 2), ("X", 3, 2),
-    ("H", 1, 3), ("E", 1, 3), ("F", 2, 1), ("F", 3, 3), ("X", 0, 2), ("F", 0, 1), ("X", 1, 3),
-    ("F", 3, 1), ("F", 1, 0), ("F", 2, 2), ("F", 3, 2), ("F", 0, 2), ("F", 1, 3),
+    ("S", 1, 0), ("Z", 1, 3), ("S", 3, 0), ("Z", 3, 3), ("S", 0, 0), ("Z", 2, 1), ("S", 2, 0),
+    ("Z", 1, 2), ("Z", 3, 2), ("P", 1, 0), ("S", 1, 3), ("S", 0, 1), ("P", 3, 0), ("S", 3, 3),
+    ("S", 1, 1), ("C", 1, 0), ("S", 2, 1), ("P", 0, 0), ("C", 3, 0), ("Z", 2, 2), ("P", 2, 0),
+    ("S", 3, 1), ("C", 0, 0), ("C", 2, 0), ("Z", 3, 1), ("P", 1, 3), ("P", 0, 1), ("C", 1, 3),
+    ("P", 3, 3), ("C", 0, 1), ("Z", 0, 3), ("P", 1, 1), ("Z", 1, 1), ("P", 2, 1), ("C", 3, 3),
+    ("Z", 2, 3), ("S", 3, 2), ("P", 3, 1), ("C", 1, 1), ("C", 2, 1), ("Z", 0, 2), ("S", 0, 2),
+    ("C", 3, 1), ("S", 2, 2), ("S", 1, 2), ("S", 0, 3), ("S", 2, 3), ("P", 3, 2), ("C", 3, 2),
+    ("R", 1, 3), ("P", 0, 2), ("P", 2, 2), ("P", 1, 2), ("C", 0, 2), ("R", 3, 3), ("P", 0, 3),
+    ("C", 2, 2), ("Z", 0, 1), ("C", 1, 2), ("P", 2, 3), ("R", 3, 2), ("C", 0, 3), ("C", 2, 3),
+    ("R", 0, 2), ("R", 2, 2), ("R", 1, 2), ("R", 2, 3), ("A", 3, 0), ("E", 3, 0), ("A", 1, 0),
+    ("E", 1, 0), ("X", 3, 0), ("R", 0, 3), ("X", 1, 0), ("A", 2, 0), ("E", 2, 0), ("H", 3, 1),
+    ("E", 3, 1), ("H", 3, 3), ("E", 3, 3), ("H", 0, 1), ("E", 0, 1), ("X", 2, 0), ("X", 3, 1),
+    ("H", 1, 3), ("E", 1, 3), ("X", 3, 3), ("F", 3, 0), ("X", 0, 1), ("H", 2, 1), ("E", 2, 1),
+    ("X", 1, 3), ("F", 1, 0), ("H", 1, 1), ("E", 1, 1), ("A", 0, 0), ("E", 0, 0), ("X", 2, 1),
+    ("H", 2, 3), ("E", 2, 3), ("X", 1, 1), ("F", 2, 0), ("H", 3, 2), ("E", 3, 2), ("X", 0, 0),
+    ("F", 3, 1), ("X", 2, 3), ("H", 0, 2), ("E", 0, 2), ("F", 3, 3), ("X", 3, 2), ("H", 2, 2),
+    ("E", 2, 2), ("X", 0, 2), ("H", 1, 2), ("E", 1, 2), ("F", 1, 3), ("X", 2, 2), ("H", 0, 3),
+    ("F", 2, 1), ("E", 0, 3), ("F", 0, 1), ("F", 1, 1), ("X", 1, 2), ("F", 0, 0), ("X", 0, 3),
+    ("F", 2, 3), ("F", 3, 2), ("F", 0, 2), ("F", 2, 2), ("F", 1, 2), ("F", 0, 3),
 )
 
 

time: 54.3 us -> 60.2 us (1.11)
  Pallas kernels: 53.3 us -> 59.2 us
    pallas_call x1, Pallas kernels: 53.3 us -> 59.2 us  [stationary_body(): pl.pallas_call(functools.partial(kernel, nb, nt), out_shape=pltpu.VMEM((r...]
where the time goes in v5:
time: 60.2 us; the launch traced here: 60 us
  Pallas kernels  59.2 us (98%)
  local copies, waits for them, and re-layouts  0.77 us (1%)
    pallas_call x1, Pallas kernels, stationary_body(): pl.pallas_call(functools.partial(kernel, nb, nt), out_shape=pltpu.VMEM((r...  59.2 us

profile of v5, /device:TPU:0, one launch (start us, length us, event | category | flops | bytes accessed | tf_op | source)
XLA Modules:
  0.0 60.0 jit_solution(16702585680931117012)
XLA Ops:
  0.0 59.2 %shard_map.64 = bf16[64,3584]{1,0:T(8,128)(2,1)S(1)} custom-call(bf16[64,3584]{1,0:T(8,128)(2,1)} %tok_hbm.1, s32[1,64]{1,0:T(1,128)} %bitcast.2, f32[1,64]{1,0:T(1,128)} %bitcast.3, bf16[2,896,256]{2,1,0:T(8,128)(2,1)} %wg_hbm.1, bf16[2,896,256]{2,1,0:T(8,128)(2,1)} %wu_hbm.1, bf16[2,256,896]{2,1,0:T(8,128)(2,1)} %wd_hbm.1), custom_call_target="tpu_custom_call" | custom-call | tf_op jit(solution)/shard_map/pallas_call | solution.py:386
  59.3 0.8 %copy.8 = bf16[64,3584]{1,0:T(8,128)(2,1)} copy(bf16[64,3584]{1,0:T(8,128)(2,1)S(1)} %shard_map.64) | data formatting | bytes 917504
